TPU v7x, 128 devices: a whole 4x4x4 slice. The times are simulated.
128 devices in a mesh: rep: 2 (over core), dp: 64 (over x, y, z).
Axes of the slice: x: 4, y: 4, z: 4, core: 2. Of those that a mesh axis runs over, the one named last changes fastest.
Arguments:
- a: bfloat16 [128, 2, 4096, 1024], P(('rep', 'dp')), parts along dimension 0
- g: bfloat16 [128, 2, 4096, 3328], P(('rep', 'dp')), parts along dimension 0
Outputs:
- output: bfloat16 [4, 1024, 3328], P('rep'), parts along dimension 0
There are 2 independent parts. A program takes and returns all parts, laid end to end along the dimension named above; each array names one.
All inputs are finite; a program needn't handle non-finite values.
Results may differ from a plain program's by a relative error of at most 0.012.
Values are sent between devices in bfloat16 or wider.
A program may use at most 1.5 GiB of HBM per device.

v0:
```python
import jax
import jax.numpy as jnp


def solution(mesh):
    groups = mesh.shape["rep"]

    def step(a, g):
        a, g = (t.reshape(groups, -1, *t.shape[1:]) for t in (a, g))
        sums = jnp.einsum("rsntd,rsntf->rndf", a, g, preferred_element_type=jnp.float32)
        return sums.astype(jnp.bfloat16).reshape(-1, *sums.shape[2:])

    return step
```

profile of v0, /device:TPU:0, one launch (start us, length us, event | category | flops | bytes accessed | tf_op | source)
XLA Modules:
  0.0 676.0 jit_solution(5646134087656519714)
XLA Ops:
  0.0 68.6 %fusion.3 = f32[1,2,1024,3328]{3,2,1,0:T(8,128)} fusion(bf16[1,2,4096,3328]{3,2,1,0:T(8,128)(2,1)} %param.1, bf16[1,2,4096,1024]{3,2,1,0:T(8,128)(2,1)} %param), kind=kOutput, calls=%fused_computation.4 | convolution fusion | flops 55834574848 | bytes 98566144 | tf_op jit(solution)/rsntd,rsntf->rndf/dot_general | solution.py:10
  68.6 607.4 %all-reduce.2 = bf16[1,2,1024,3328]{3,2,1,0:T(8,128)(2,1)} all-reduce(f32[1,2,1024,3328]{3,2,1,0:T(8,128)} %fusion.3), channel_id=1, replica_groups=[2,64]<=[128], use_global_device_ids=true, to_apply=%add.clone | all-reduce | flops 6815744 | bytes 40894464 | tf_op jit(solution)/rsntd,rsntf->rndf/dot_general | solution.py:10
where the time goes:
time: 676 us
  blocking collectives  607 us (90%)
  matrix products  68.6 us (10%)
    dot_general x1, blocking collectives, step(): jnp.einsum('rsntd,rsntf->rndf', a, g, preferred_element_type=jnp.float32)  607 us
    dot_general x1, matrix products, step(): jnp.einsum('rsntd,rsntf->rndf', a, g, preferred_element_type=jnp.float32)  68.6 us

commit v1 on v0

v1 whole, which is shorter than its diff:
```python
import jax
import jax.numpy as jnp
from jax import lax
from jax.experimental import pallas as pl
from jax.experimental.pallas import tpu as pltpu
from jax.sharding import PartitionSpec as P

MESH = pl.DeviceIdType.MESH
F32, BF16 = jnp.float32, jnp.bfloat16
WIDTH = 256
LANES = 128
SLOTS = 6
SIDE = 4
STRIDE = (16, 4, 1)
CHUNK = (256, 64, 16)
TOKENS_AT_ONCE = 512
ROWS_AT_ONCE = 512

OFFSET = (1, 3, 5, 6, 7, 8, 9, 10, 11, 12, 13, 15, 17)


def kernel(
    a_hbm, g_hbm, out_hbm,
    a_in, a_t, g_in, tb0, tb1, tb2, tf1, tf2, mid0, mid1, mid2, got0, got1, got2, sums,
    a_sem, g_sem, o_sem, rs_send, rs_recv, ag_send, ag_recv,
):
    matrices, tokens, rows = a_hbm.shape[1], a_hbm.shape[2], a_hbm.shape[3]
    per_matrix = g_hbm.shape[3] // WIDTH
    units = matrices * per_matrix
    parts = tokens // TOKENS_AT_ONCE

    rep, me = lax.axis_index("rep"), lax.axis_index("dp")
    pos = tuple(lax.rem(me // s, SIDE) for s in STRIDE)

    def neighbour(axis, step):
        return me + (lax.rem(pos[axis] + step + SIDE, SIDE) - pos[axis]) * STRIDE[axis]

    right = tuple(neighbour(axis, 1) for axis in range(3))
    left = tuple(neighbour(axis, -1) for axis in range(3))

    tb, tf, mid, got = (tb0, tb1, tb2), (None, tf1, tf2), (mid0, mid1, mid2), (got0, got1, got2)

    def span(block, size):
        return pl.ds(pl.multiple_of(block * size, size), size)

    def put(src, dst, send, recv, device):
        return pltpu.make_async_remote_copy(
            src_ref=src, dst_ref=dst, send_sem=send, recv_sem=recv, device_id=(rep, device), device_id_type=MESH
        )

    def rs_put(src, u, c, p, kind, way):
        slot = lax.rem(u, SLOTS)
        device = (right, left)[way][(c + p) % 3]
        return put(
            src, got[p].at[u, kind, way], rs_send.at[slot, p, kind, way], rs_recv.at[u, p, kind, way], device
        )

    def rs_first(u, c, p):
        i, own = pos[(c + p) % 3], tb[p].at[lax.rem(u, SLOTS)]
        after, over, before = (span(lax.rem(i + k, SIDE), CHUNK[p]) for k in (1, 2, 3))
        return (
            rs_put(own.at[1, over], u, c, p, 0, 0),
            rs_put(own.at[0, over], u, c, p, 0, 1),
            rs_put(own.at[0, after], u, c, p, 1, 0),
            rs_put(own.at[1, before], u, c, p, 1, 1),
        )

    def rs_second(u, c, p):
        slot = lax.rem(u, SLOTS)
        return tuple(rs_put(mid[p].at[slot, way], u, c, p, 2, way) for way in (0, 1))

    def own_term(u, p, half, block):
        own = (tb[0] if p == 0 else tf[p])[lax.rem(u, SLOTS), half, span(block, CHUNK[p])]
        return own.astype(F32)

    def rs_middle(u, c, p):
        i, slot = pos[(c + p) % 3], lax.rem(u, SLOTS)
        copies = rs_first(u, c, p)
        for copy in copies[:2]:
            copy.wait_recv()
        for copy in copies:
            copy.wait_send()
        for way, half, step in ((0, 1, 1), (1, 0, 3)):
            total = own_term(u, p, half, lax.rem(i + step, SIDE)) + got[p][u, 0, way].astype(F32)
            mid[p][slot, way] = total.astype(BF16)

    def block_rows(c, p):
        first = 0
        for q in range(p):
            first = first + pos[(c + q) % 3] * CHUNK[q]
        return first

    def blk(c, p, step):
        first = block_rows(c, p) + lax.rem(pos[(c + p) % 3] + step, SIDE) * CHUNK[p]
        return pl.ds(pl.multiple_of(first, CHUNK[p]), CHUNK[p])

    def rs_end(u, c, p):
        i, slot = pos[(c + p) % 3], lax.rem(u, SLOTS)
        for copy in rs_first(u, c, p)[2:]:
            copy.wait_recv()
        for copy in rs_second(u, c, p):
            copy.wait_recv()
            copy.wait_send()
        for half in (0, 1):
            total = own_term(u, p, half, i) + got[p][u, 1, half].astype(F32) + got[p][u, 2, 1 - half].astype(F32)
            if p < 2:
                tf[p + 1][slot, half] = total
                tb[p + 1][slot, half] = total.astype(BF16)
            else:
                sums[u, half, blk(c, p, 0)] = total.astype(BF16)

    def ag_put(ref, u, c, p, step, way):
        slot = lax.rem(u, SLOTS)
        device = (right, left)[way][(c + p) % 3]
        return put(ref, ref, ag_send.at[slot, p, step, way], ag_recv.at[u, p, step, way], device)

    def ag_first(u, c, p):
        return tuple(ag_put(sums.at[u, :, blk(c, p, 0)], u, c, p, 0, way) for way in (0, 1))

    def ag_second(u, c, p):
        return (
            ag_put(sums.at[u, 0, blk(c, p, 3)], u, c, p, 1, 0),
            ag_put(sums.at[u, 1, blk(c, p, 1)], u, c, p, 1, 1),
        )

    def start(copies):
        for copy in copies:
            copy.start()

    def wait(copies):
        for copy in copies:
            copy.wait_recv()
            copy.wait_send()

    def out_copies(u):
        n, j = u // per_matrix, lax.rem(u, per_matrix)
        return tuple(
            pltpu.make_async_copy(
                sums.at[u, half],
                out_hbm.at[n, :, pl.ds(pl.multiple_of(j * WIDTH + half * LANES, LANES), LANES)],
                o_sem.at[u, half],
            )
            for half in (0, 1)
        )

    stages = (
        (lambda u, c: None, lambda u, c: start(rs_first(u, c, 0))),
        (lambda u, c: rs_middle(u, c, 0), lambda u, c: start(rs_second(u, c, 0))),
        (lambda u, c: rs_end(u, c, 0), lambda u, c: start(rs_first(u, c, 1))),
        (lambda u, c: rs_middle(u, c, 1), lambda u, c: start(rs_second(u, c, 1))),
        (lambda u, c: rs_end(u, c, 1), lambda u, c: start(rs_first(u, c, 2))),
        (lambda u, c: rs_middle(u, c, 2), lambda u, c: start(rs_second(u, c, 2))),
        (lambda u, c: rs_end(u, c, 2), lambda u, c: start(ag_first(u, c, 2))),
        (lambda u, c: wait(ag_first(u, c, 2)), lambda u, c: start(ag_second(u, c, 2))),
        (lambda u, c: wait(ag_second(u, c, 2)), lambda u, c: start(ag_first(u, c, 1))),
        (lambda u, c: wait(ag_first(u, c, 1)), lambda u, c: start(ag_second(u, c, 1))),
        (lambda u, c: wait(ag_second(u, c, 1)), lambda u, c: start(ag_first(u, c, 0))),
        (lambda u, c: wait(ag_first(u, c, 0)), lambda u, c: start(ag_second(u, c, 0))),
        (lambda u, c: wait(ag_second(u, c, 0)), lambda u, c: start(out_copies(u))),
    )

    def a_copy(n, part):
        return pltpu.make_async_copy(
            a_hbm.at[0, n, span(part, TOKENS_AT_ONCE)], a_in.at[part], a_sem.at[part]
        )

    def g_copy(u):
        n, j, slot = u // per_matrix, lax.rem(u, per_matrix), lax.rem(u, 2)
        return pltpu.make_async_copy(g_hbm.at[0, n, :, span(j, WIDTH)], g_in.at[slot], g_sem.at[slot])

    def load_a(n):
        def one(part, _):
            a_copy(n, part).wait()
            for column in range(0, rows, 256):
                block = a_in[part, :, column : column + 256]
                a_t[column : column + 256, span(part, TOKENS_AT_ONCE)] = block.T
            return 0

        lax.fori_loop(0, parts, one, 0)

    def fetch_a(n):
        def one(part, _):
            a_copy(n, part).start()
            return 0

        lax.fori_loop(0, parts, one, 0)

    def multiply(u):
        g_copy(u).wait()

        @pl.when(u + 1 < units)
        def _():
            g_copy(u + 1).start()

        def one(m, _):
            at = span(m, ROWS_AT_ONCE)
            term = jnp.dot(a_t[at, :], g_in[lax.rem(u, 2)], preferred_element_type=F32).astype(BF16)
            for half in (0, 1):
                tb0[lax.rem(u, SLOTS), half, at] = term[:, half * LANES : (half + 1) * LANES]
            return 0

        lax.fori_loop(0, rows // ROWS_AT_ONCE, one, 0)

    fetch_a(0)
    g_copy(0).start()

    barrier = pltpu.get_barrier_semaphore()
    for device in right + left:
        pl.semaphore_signal(barrier, inc=1, device_id=(rep, device), device_id_type=MESH)
    pl.semaphore_wait(barrier, 6)

    ticks = units + OFFSET[-1]

    def three(group, _):
        for s in range(3):
            t = group * 3 + s
            later = None

            def stage(k, which):
                u, c = t - OFFSET[k], (s - OFFSET[k]) % 3

                @pl.when(jnp.logical_and(u >= 0, u < units))
                def _():
                    stages[k][which](u, c)

            for k in range(len(stages)):
                stage(k, 0)
                if later is not None:
                    stage(later, 1)
                later = k
            stage(later, 1)

            for n in range(matrices):
                if (n * per_matrix) % 3 == s:

                    @pl.when(t == n * per_matrix)
                    def _(n=n):
                        load_a(n)
                        if n + 1 < matrices:
                            fetch_a(n + 1)

            @pl.when(t < units)
            def _():
                multiply(t)

        return 0

    lax.fori_loop(0, (ticks + 3) // 3, three, 0)

    def last(u, _):
        for copy in out_copies(u):
            copy.wait()
        return 0

    lax.fori_loop(0, units, last, 0)


def sum_kernel(a, g):
    _, matrices, tokens, rows = a.shape
    columns = g.shape[3]
    units = matrices * columns // WIDTH
    dma = pltpu.SemaphoreType.DMA
    return pl.pallas_call(
        kernel,
        out_shape=jax.ShapeDtypeStruct((matrices, rows, columns), BF16),
        in_specs=[pl.BlockSpec(memory_space=pl.ANY)] * 2,
        out_specs=pl.BlockSpec(memory_space=pl.ANY),
        scratch_shapes=[
            pltpu.VMEM((tokens // TOKENS_AT_ONCE, TOKENS_AT_ONCE, rows), BF16),
            pltpu.VMEM((rows, tokens), BF16),
            pltpu.VMEM((2, tokens, WIDTH), BF16),
            pltpu.VMEM((SLOTS, 2, rows, LANES), BF16),
            pltpu.VMEM((SLOTS, 2, CHUNK[0], LANES), BF16),
            pltpu.VMEM((SLOTS, 2, CHUNK[1], LANES), BF16),
            pltpu.VMEM((SLOTS, 2, CHUNK[0], LANES), F32),
            pltpu.VMEM((SLOTS, 2, CHUNK[1], LANES), F32),
            *(pltpu.VMEM((SLOTS, 2, size, LANES), BF16) for size in CHUNK),
            *(pltpu.VMEM((units, 3, 2, size, LANES), BF16) for size in CHUNK),
            pltpu.VMEM((units, 2, rows, LANES), BF16),
            dma((tokens // TOKENS_AT_ONCE,)),
            dma((2,)),
            dma((units, 2)),
            dma((SLOTS, 3, 3, 2)),
            dma((units, 3, 3, 2)),
            dma((SLOTS, 3, 2, 2)),
            dma((units, 3, 2, 2)),
        ],
        compiler_params=pltpu.CompilerParams(
            collective_id=0, has_side_effects=True, vmem_limit_bytes=67_000_000
        ),
        name="sum_of_products",
    )(a, g)


def solution(mesh):
    return jax.shard_map(
        sum_kernel,
        mesh=mesh,
        in_specs=(P(("rep", "dp")), P(("rep", "dp"))),
        out_specs=P("rep"),
        check_vma=False,
    )
```

time: 676 us -> 193 us (0.29)
  blocking collectives: 607 us -> 0 us
  Pallas kernels: 0 us -> 181 us
  matrix products: 68.6 us -> 0 us
  local copies, waits for them, and re-layouts: 0 us -> 12.1 us
    dot_general x1 -> x0, blocking collectives: 607 us -> none  [step(): jnp.einsum('rsntd,rsntf->rndf', a, g, preferred_element_type=jnp.float32)]
    pallas_call x0 -> x1, Pallas kernels: none -> 181 us  [sum_kernel(): pl.pallas_call(kernel, out_shape=jax.ShapeDtypeStruct((matrices, rows, co...]
    dot_general x1 -> x0, matrix products: 68.6 us -> none  [step(): jnp.einsum('rsntd,rsntf->rndf', a, g, preferred_element_type=jnp.float32)]
    unnamed x0 -> x1, local copies, waits for them, and re-layouts: none -> 12.1 us
where the time goes in v1:
time: 193 us
  Pallas kernels  181 us (94%)
  local copies, waits for them, and re-layouts  12.1 us (6%)
    pallas_call x1, Pallas kernels, sum_kernel(): pl.pallas_call(kernel, out_shape=jax.ShapeDtypeStruct((matrices, rows, co...  181 us
    unnamed x1, local copies, waits for them, and re-layouts  12.1 us

profile of v1, /device:TPU:0, one launch (start us, length us, event | category | flops | bytes accessed | tf_op | source)
XLA Modules:
  0.0 192.8 jit_solution(12952496555462494810)
XLA Ops:
  0.0 180.7 %sum_of_products.1 = bf16[2,1024,3328]{2,1,0:T(8,128)(2,1)} custom-call(bf16[1,2,4096,1024]{3,2,1,0:T(8,128)(2,1)} %a_hbm.1, bf16[1,2,4096,3328]{3,2,1,0:T(8,128)(2,1)} %g_hbm.1), custom_call_target="tpu_custom_call" | custom-call | tf_op jit(solution)/shard_map/sum_of_products/pallas_call | solution.py:263
  180.7 12.1 %copy.4 = bf16[2,1024,3328]{2,1,0:T(8,128)(2,1)} copy(bf16[2,1024,3328]{2,1,0:T(8,128)(2,1)} %sum_of_products.1) | data formatting | bytes 27262976

commit v2 on v1

--- a/solution.py
+++ b/solution.py
@@ -16,13 +16,14 @@
 TOKENS_AT_ONCE = 512
 ROWS_AT_ONCE = 512
 
-OFFSET = (1, 3, 5, 6, 7, 8, 9, 10, 11, 12, 13, 15, 17)
+OFFSET = (1, 3, 5, 6, 7, 9, 10, 12, 13, 15, 17, 22, 27)
+ORDER = (7, 2, 5, 12, 9, 1, 8, 0, 11, 3, 6, 4, 10)
 
 
 def kernel(
-    a_hbm, g_hbm, out_hbm,
-    a_in, a_t, g_in, tb0, tb1, tb2, tf1, tf2, mid0, mid1, mid2, got0, got1, got2, sums,
-    a_sem, g_sem, o_sem, rs_send, rs_recv, ag_send, ag_recv,
+    a_hbm, g_hbm, sums,
+    a_in, a_t, g_in, tb0, tb1, tb2, tf1, tf2, mid0, mid1, mid2, got0, got1, got2,
+    a_sem, g_sem, rs_send, rs_recv, ag_send, ag_recv,
 ):
     matrices, tokens, rows = a_hbm.shape[1], a_hbm.shape[2], a_hbm.shape[3]
     per_matrix = g_hbm.shape[3] // WIDTH
@@ -132,17 +133,6 @@
             copy.wait_recv()
             copy.wait_send()
 
-    def out_copies(u):
-        n, j = u // per_matrix, lax.rem(u, per_matrix)
-        return tuple(
-            pltpu.make_async_copy(
-                sums.at[u, half],
-                out_hbm.at[n, :, pl.ds(pl.multiple_of(j * WIDTH + half * LANES, LANES), LANES)],
-                o_sem.at[u, half],
-            )
-            for half in (0, 1)
-        )
-
     stages = (
         (lambda u, c: None, lambda u, c: start(rs_first(u, c, 0))),
         (lambda u, c: rs_middle(u, c, 0), lambda u, c: start(rs_second(u, c, 0))),
@@ -156,7 +146,7 @@
         (lambda u, c: wait(ag_first(u, c, 1)), lambda u, c: start(ag_second(u, c, 1))),
         (lambda u, c: wait(ag_second(u, c, 1)), lambda u, c: start(ag_first(u, c, 0))),
         (lambda u, c: wait(ag_first(u, c, 0)), lambda u, c: start(ag_second(u, c, 0))),
-        (lambda u, c: wait(ag_second(u, c, 0)), lambda u, c: start(out_copies(u))),
+        (lambda u, c: wait(ag_second(u, c, 0)), lambda u, c: None),
     )
 
     def a_copy(n, part):
@@ -223,7 +213,7 @@
                 def _():
                     stages[k][which](u, c)
 
-            for k in range(len(stages)):
+            for k in ORDER:
                 stage(k, 0)
                 if later is not None:
                     stage(later, 1)
@@ -247,12 +237,28 @@
 
     lax.fori_loop(0, (ticks + 3) // 3, three, 0)
 
-    def last(u, _):
-        for copy in out_copies(u):
-            copy.wait()
+
+def store_kernel(sums, out_hbm, sem):
+    units = sums.shape[0]
+    per_matrix = units // out_hbm.shape[0]
+
+    def copy(u, half):
+        n, j = u // per_matrix, lax.rem(u, per_matrix)
+        at = pl.ds(pl.multiple_of(j * WIDTH + half * LANES, LANES), LANES)
+        return pltpu.make_async_copy(sums.at[u, half], out_hbm.at[n, :, at], sem.at[u, half])
+
+    def begin(u, _):
+        for half in (0, 1):
+            copy(u, half).start()
         return 0
 
-    lax.fori_loop(0, units, last, 0)
+    def end(u, _):
+        for half in (0, 1):
+            copy(u, half).wait()
+        return 0
+
+    lax.fori_loop(0, units, begin, 0)
+    lax.fori_loop(0, units, end, 0)
 
 
 def sum_kernel(a, g):
@@ -260,11 +266,11 @@
     columns = g.shape[3]
     units = matrices * columns // WIDTH
     dma = pltpu.SemaphoreType.DMA
-    return pl.pallas_call(
+    sums = pl.pallas_call(
         kernel,
-        out_shape=jax.ShapeDtypeStruct((matrices, rows, columns), BF16),
+        out_shape=pltpu.VMEM((units, 2, rows, LANES), BF16),
         in_specs=[pl.BlockSpec(memory_space=pl.ANY)] * 2,
-        out_specs=pl.BlockSpec(memory_space=pl.ANY),
+        out_specs=pl.BlockSpec(memory_space=pltpu.VMEM),
         scratch_shapes=[
             pltpu.VMEM((tokens // TOKENS_AT_ONCE, TOKENS_AT_ONCE, rows), BF16),
             pltpu.VMEM((rows, tokens), BF16),
@@ -276,20 +282,27 @@
             pltpu.VMEM((SLOTS, 2, CHUNK[1], LANES), F32),
             *(pltpu.VMEM((SLOTS, 2, size, LANES), BF16) for size in CHUNK),
             *(pltpu.VMEM((units, 3, 2, size, LANES), BF16) for size in CHUNK),
-            pltpu.VMEM((units, 2, rows, LANES), BF16),
             dma((tokens // TOKENS_AT_ONCE,)),
             dma((2,)),
-            dma((units, 2)),
             dma((SLOTS, 3, 3, 2)),
             dma((units, 3, 3, 2)),
             dma((SLOTS, 3, 2, 2)),
             dma((units, 3, 2, 2)),
         ],
         compiler_params=pltpu.CompilerParams(
-            collective_id=0, has_side_effects=True, vmem_limit_bytes=67_000_000
+            collective_id=0, has_side_effects=True, vmem_limit_bytes=52_000_000
         ),
         name="sum_of_products",
     )(a, g)
+    return pl.pallas_call(
+        store_kernel,
+        out_shape=jax.ShapeDtypeStruct((matrices, rows, columns), BF16),
+        in_specs=[pl.BlockSpec(memory_space=pltpu.VMEM)],
+        out_specs=pl.BlockSpec(memory_space=pl.ANY),
+        scratch_shapes=[dma((units, 2))],
+        compiler_params=pltpu.CompilerParams(vmem_limit_bytes=1 << 20),
+        name="store",
+    )(sums)
 
 
 def solution(mesh):

time: 193 us -> 161 us (0.83)
  Pallas kernels: 181 us -> 161 us
  local copies, waits for them, and re-layouts: 12.1 us -> 0 us
    pallas_call x1 -> x2, Pallas kernels: 181 us -> 161 us  [the longest x1 156 us: sum_kernel(): pl.pallas_call(kernel, out_shape=pltpu.VMEM((units, 2, rows, LANES), BF16...]
    unnamed x1 -> x0, local copies, waits for them, and re-layouts: 12.1 us -> none
where the time goes in v2:
time: 161 us
  Pallas kernels  161 us (100%)
    pallas_call x1, Pallas kernels, sum_kernel(): pl.pallas_call(kernel, out_shape=pltpu.VMEM((units, 2, rows, LANES), BF16...  156 us
    pallas_call x1, Pallas kernels, sum_kernel(): pl.pallas_call(store_kernel, out_shape=jax.ShapeDtypeStruct((matrices, ro...  5.3 us

profile of v2, /device:TPU:0, one launch (start us, length us, event | category | flops | bytes accessed | tf_op | source)
XLA Modules:
  0.0 160.8 jit_solution(4485270216770670982)
XLA Ops:
  0.0 155.5 %sum_of_products.1.sums = bf16[26,2,1024,128]{3,2,1,0:T(8,128)(2,1)S(1)} custom-call(bf16[1,2,4096,1024]{3,2,1,0:T(8,128)(2,1)} %a_hbm.1, bf16[1,2,4096,3328]{3,2,1,0:T(8,128)(2,1)} %g_hbm.1), custom_call_target="tpu_custom_call" | custom-call | tf_op jit(solution)/shard_map/sum_of_products/pallas_call | solution.py:269
  155.6 5.3 %store.1 = bf16[2,1024,3328]{2,1,0:T(8,128)(2,1)} custom-call(bf16[26,2,1024,128]{3,2,1,0:T(8,128)(2,1)S(1)} %sum_of_products.1.sums), custom_call_target="tpu_custom_call" | custom-call | tf_op jit(solution)/shard_map/store/pallas_call | solution.py:297

commit v3 on v0

v3 whole, which is shorter than its diff:
```python
import functools

import jax
import jax.numpy as jnp
from jax import lax
from jax.experimental import pallas as pl
from jax.experimental.pallas import tpu as pltpu
from jax.sharding import PartitionSpec as P

MESH = pl.DeviceIdType.MESH
F32, BF16 = jnp.float32, jnp.bfloat16
WIDTH = 256
LANES = 128
SIDE = 4
STRIDE = (16, 4, 1)
CHUNK = (256, 64)
TOKENS_AT_ONCE = 512
TERM_SLOTS = 8
SUM_SLOTS = 12
DELTA = 1

OFFSET = (1, 3, 5, 7, 9, 10, 13, 15, 17, 29, 33)
ORDER = (10, 4, 3, 2, 7, 6, 1, 0, 8, 9, 5)
LOOPED = 27
DRAIN = (
    (9, 2), (3, 21), (5, 18), (1, 25), (2, 23), (6, 15), (9, 5), (3, 22), (4, 19), (7, 14), (6, 16), (9, 4), (4, 20),
    (4, 21), (6, 17), (3, 23), (4, 22), (2, 24), (2, 25), (6, 18), (9, 1), (9, 6), (5, 19), (8, 12), (7, 16), (5, 21),
    (7, 17), (5, 20), (3, 24), (7, 13), (7, 15), (4, 23), (7, 18), (3, 25), (10, 5), (9, 0), (9, 10), (8, 11),
    (5, 22), (8, 16), (9, 7), (4, 24), (4, 25), (6, 21), (6, 20), (9, 3), (5, 23), (6, 19), (9, 8), (8, 18), (5, 24),
    (6, 22), (5, 25), (7, 19), (10, 6), (8, 15), (8, 13), (8, 17), (7, 21), (6, 23), (7, 20), (6, 24), (10, 10),
    (6, 25), (7, 22), (9, 18), (8, 14), (8, 19), (7, 23), (7, 24), (10, 7), (8, 21), (8, 20), (7, 25), (9, 13),
    (9, 14), (8, 22), (8, 24), (8, 23), (10, 0), (9, 12), (9, 11), (8, 25), (9, 21), (9, 16), (9, 17), (10, 3),
    (9, 9), (9, 22), (9, 15), (9, 20), (10, 4), (10, 18), (9, 24), (10, 2), (9, 19), (10, 1), (10, 8), (9, 23),
    (10, 11), (9, 25), (10, 19), (10, 16), (10, 20), (10, 17), (10, 21), (10, 9), (10, 15), (10, 13), (10, 14),
    (10, 12), (10, 22), (10, 25), (10, 23), (10, 24),
)


def kernel(
    a_hbm, g_hbm, sums,
    a_in, a_t, g_in, tb0, tb1, tf1, mid0, mid1, got0, got1, parts_in,
    a_sem, g_sem, rs_send, rs_recv, ag_send, ag_recv,
):
    _, matrices, tokens, rows = a_hbm.shape
    per_matrix = g_hbm.shape[3] // WIDTH
    units = matrices * per_matrix
    pieces = tokens // TOKENS_AT_ONCE

    rep, me = lax.axis_index("rep"), lax.axis_index("dp")
    pos = tuple(lax.rem(me // s, SIDE) for s in STRIDE)

    def neighbour(axis, step):
        return me + (lax.rem(pos[axis] + step + SIDE, SIDE) - pos[axis]) * STRIDE[axis]

    right = tuple(neighbour(axis, 1) for axis in range(3))
    left = tuple(neighbour(axis, -1) for axis in range(3))

    tb, mid, got = (tb0, tb1), (mid0, mid1), (got0, got1)
    slots = (TERM_SLOTS, SUM_SLOTS)

    def axis_of(u, h, p):
        return (u[1] + h * DELTA + p) % 3

    def place(u, h, p):
        return pos[axis_of(u, h, p)]

    def device(u, h, p, way):
        return (right, left)[way][axis_of(u, h, p)]

    def slot(u, p):
        return lax.rem(u[0], slots[p])

    def turn(i, step):
        return lax.rem(i + step % SIDE, SIDE)

    def span(block, size, first=0):
        return pl.ds(pl.multiple_of(first + block * size, size), size)

    def put(src, dst, send, recv, u, h, p, way):
        return pltpu.make_async_remote_copy(
            src_ref=src,
            dst_ref=dst,
            send_sem=send,
            recv_sem=recv,
            device_id=(rep, device(u, h, p, way)),
            device_id_type=MESH,
        )

    def arrive(sem, like):
        pltpu.make_async_copy(like, like, sem).wait()

    def scatter_put(u, h, p, kind):
        if kind == 2:
            src = mid[p].at[slot(u, 1), h]
        else:
            step = 2 if kind == 0 else 1 - 2 * h
            src = tb[p].at[slot(u, p), h, span(turn(place(u, h, p), step), CHUNK[p])]
        send = rs_send.at[p, kind // 2, slot(u, 1)]
        recv = rs_recv.at[u[0], p, min(kind, 1)]
        return put(src, got[p].at[u[0], kind, h], send, recv, u, h, p, h if kind == 1 else 1 - h)

    def gather_ref(u, h, p, step):
        i = turn(place(u, h, p), step)
        if p == 2:
            return parts_in.at[u[0], h, i]
        first = place(u, h, 0) * CHUNK[0] if p == 1 else 0
        return sums.at[u[0], h, span(i, CHUNK[p], first)]

    def gather_put(u, h, p, kind):
        ref = gather_ref(u, h, p, (2 * h - 1) if kind == 2 else 0)
        send, recv = ag_send.at[u[0], p], ag_recv.at[u[0], p, min(kind, 1)]
        return put(ref, ref, send, recv, u, h, p, 1 - h if kind == 1 else h)

    def own_term(u, h, p, block):
        own = (tb0 if p == 0 else tf1)[slot(u, p), h, span(block, CHUNK[p])]
        return own.astype(F32)

    both = (0, 1)

    def scatter_send(u, p):
        for kind in (0, 1):
            for h in both:
                scatter_put(u, h, p, kind).start()

    def scatter_mid(u, p):
        arrive(rs_recv.at[u[0], p, 0], got[p].at[u[0], 0])
        for h in both:
            block = turn(place(u, h, p), 2 * h - 1)
            total = own_term(u, h, p, block) + got[p][u[0], 0, h].astype(F32)
            mid[p][slot(u, 1), h] = total.astype(BF16)

    def scatter_pass(u, p):
        for h in both:
            scatter_put(u, h, p, 2).start()

    def scatter_end(u, p):
        arrive(rs_recv.at[u[0], p, 1], got[p].at[u[0], 1:3])
        arrive(rs_send.at[p, 0, slot(u, 1)], got[p].at[u[0], 0:2])
        arrive(rs_send.at[p, 1, slot(u, 1)], got[p].at[u[0], 2])
        for h in both:
            i = place(u, h, p)
            total = own_term(u, h, p, i) + got[p][u[0], 1, h].astype(F32) + got[p][u[0], 2, h].astype(F32)
            if p == 0:
                tf1[slot(u, 1), h] = total
                tb1[slot(u, 1), h] = total.astype(BF16)
            else:
                parts_in[u[0], h, place(u, h, 2)] = total.astype(BF16)

    def gather_send(u, p):
        for kind in (0, 1):
            for h in both:
                gather_put(u, h, p, kind).start()

    def gather_pass(u, p):
        arrive(ag_recv.at[u[0], p, 0], got[min(p, 1)].at[u[0], 0])
        for h in both:
            gather_put(u, h, p, 2).start()

    def gather_end(u, p):
        arrive(ag_recv.at[u[0], p, 1], got[min(p, 1)].at[u[0], 1:3])
        arrive(ag_send.at[u[0], p], got[min(p, 1)].at[u[0]])

    def add_parts(u):
        gather_end(u, 2)
        for h in both:
            total = parts_in[u[0], h, 0].astype(F32)
            for i in range(1, SIDE):
                total = total + parts_in[u[0], h, i].astype(F32)
            first = place(u, h, 0) * CHUNK[0]
            sums[u[0], h, span(place(u, h, 1), CHUNK[1], first)] = total.astype(BF16)

    def gather_on(u):
        gather_end(u, 1)
        gather_send(u, 0)

    stages = (
        (lambda u: scatter_send(u, 0), None),
        (lambda u: scatter_mid(u, 0), lambda u: scatter_pass(u, 0)),
        (lambda u: scatter_end(u, 0), lambda u: scatter_send(u, 1)),
        (lambda u: scatter_mid(u, 1), lambda u: scatter_pass(u, 1)),
        (lambda u: scatter_end(u, 1), lambda u: gather_send(u, 2)),
        (lambda u: gather_pass(u, 2), None),
        (add_parts, lambda u: gather_send(u, 1)),
        (lambda u: gather_pass(u, 1), None),
        (gather_on, None),
        (lambda u: gather_pass(u, 0), None),
        (lambda u: gather_end(u, 0), None),
    )

    def each(first, last, f):
        def one(u, _):
            f(u)
            return 0

        lax.fori_loop(first, last, one, 0)

    def a_copy(n, piece):
        return pltpu.make_async_copy(a_hbm.at[0, n, span(piece, TOKENS_AT_ONCE)], a_in.at[piece], a_sem.at[piece])

    def g_copy(u):
        n, j, slot = u // per_matrix, lax.rem(u, per_matrix), lax.rem(u, 2)
        return pltpu.make_async_copy(g_hbm.at[0, n, :, span(j, WIDTH)], g_in.at[slot], g_sem.at[slot])

    def turn_a(piece, n):
        a_copy(n, piece).wait()
        for column in range(0, rows, 256):
            block = a_in[piece, :, column : column + 256]
            a_t[column : column + 256, span(piece, TOKENS_AT_ONCE)] = block.T

    def load_a(n):
        each(0, pieces, lambda piece: turn_a(piece, n))
        if n + 1 < matrices:
            each(0, pieces, lambda piece: a_copy(n + 1, piece).start())

    def multiply(u):
        g_copy(u).wait()

        @pl.when(u + 1 < units)
        def _():
            g_copy(u + 1).start()

        term = jnp.dot(a_t[...], g_in[lax.rem(u, 2)], preferred_element_type=F32).astype(BF16)
        for h in both:
            tb0[lax.rem(u, TERM_SLOTS), h] = term[:, h * LANES : (h + 1) * LANES]

    each(0, pieces, lambda piece: a_copy(0, piece).start())
    g_copy(0).start()
    barrier = pltpu.get_barrier_semaphore()
    for other in right + left:
        pl.semaphore_signal(barrier, inc=1, device_id=(rep, other), device_id_type=MESH)
    load_a(0)
    multiply(jnp.int32(0))
    pl.semaphore_wait(barrier, 6)

    def three(group, _):
        for s in range(3):
            t = group * 3 + s + 1
            late = None
            for k in ORDER:
                number, colour = t - OFFSET[k], (s + 1 - OFFSET[k]) % 3
                now, then = stages[k]
                due = jnp.logical_and(number >= 0, number < units)

                @pl.when(due)
                def _():
                    now((number, colour))

                if late is not None:
                    pl.when(late[0])(late[1])
                late = None if then is None else (due, functools.partial(then, (number, colour)))
            if late is not None:
                pl.when(late[0])(late[1])

            for n in range(1, matrices):
                if (n * per_matrix - 1) % 3 == s:

                    @pl.when(t == n * per_matrix)
                    def _():
                        load_a(n)

            @pl.when(t < units)
            def _():
                multiply(t)

        return 0

    lax.fori_loop(0, LOOPED // 3, three, 0)

    late = None
    for k, u in DRAIN:
        now, then = stages[k]
        now((jnp.int32(u), u % 3))
        if late is not None:
            late()
        late = None if then is None else functools.partial(then, (jnp.int32(u), u % 3))


def store_kernel(sums, out_hbm, sem):
    units = sums.shape[0]
    per_matrix = units // out_hbm.shape[0]

    def copy(u, half):
        n, j = u // per_matrix, lax.rem(u, per_matrix)
        at = pl.ds(pl.multiple_of(j * WIDTH + half * LANES, LANES), LANES)
        return pltpu.make_async_copy(sums.at[u, half], out_hbm.at[n, :, at], sem.at[u, half])

    def begin(u, _):
        for half in (0, 1):
            copy(u, half).start()
        return 0

    def end(u, _):
        for half in (0, 1):
            copy(u, half).wait()
        return 0

    lax.fori_loop(0, units, begin, 0)
    lax.fori_loop(0, units, end, 0)


def sum_products(a, g):
    _, matrices, tokens, rows = a.shape
    columns = g.shape[3]
    units = matrices * columns // WIDTH
    dma = pltpu.SemaphoreType.DMA
    sums = pl.pallas_call(
        kernel,
        out_shape=pltpu.VMEM((units, 2, rows, LANES), BF16),
        in_specs=[pl.BlockSpec(memory_space=pl.ANY)] * 2,
        out_specs=pl.BlockSpec(memory_space=pltpu.VMEM),
        scratch_shapes=[
            pltpu.VMEM((tokens // TOKENS_AT_ONCE, TOKENS_AT_ONCE, rows), BF16),
            pltpu.VMEM((rows, tokens), BF16),
            pltpu.VMEM((2, tokens, WIDTH), BF16),
            pltpu.VMEM((TERM_SLOTS, 2, rows, LANES), BF16),
            pltpu.VMEM((SUM_SLOTS, 2, CHUNK[0], LANES), BF16),
            pltpu.VMEM((SUM_SLOTS, 2, CHUNK[0], LANES), F32),
            *(pltpu.VMEM((SUM_SLOTS, 2, size, LANES), BF16) for size in CHUNK),
            *(pltpu.VMEM((units, 3, 2, size, LANES), BF16) for size in CHUNK),
            pltpu.VMEM((units, 2, SIDE, CHUNK[1], LANES), BF16),
            dma((tokens // TOKENS_AT_ONCE,)),
            dma((2,)),
            dma((2, 2, SUM_SLOTS)),
            dma((units, 2, 2)),
            dma((units, 3)),
            dma((units, 3, 2)),
        ],
        compiler_params=pltpu.CompilerParams(
            collective_id=0, has_side_effects=True, vmem_limit_bytes=53_000_000
        ),
        name="sum_of_products",
    )(a, g)
    return pl.pallas_call(
        store_kernel,
        out_shape=jax.ShapeDtypeStruct((matrices, rows, columns), BF16),
        in_specs=[pl.BlockSpec(memory_space=pltpu.VMEM)],
        out_specs=pl.BlockSpec(memory_space=pl.ANY),
        scratch_shapes=[dma((units, 2))],
        compiler_params=pltpu.CompilerParams(vmem_limit_bytes=1 << 20),
        name="store",
    )(sums)


def solution(mesh):
    return jax.shard_map(
        sum_products,
        mesh=mesh,
        in_specs=(P(("rep", "dp")), P(("rep", "dp"))),
        out_specs=P("rep"),
        check_vma=False,
    )
```

time: 676 us -> 147 us (0.22)
  blocking collectives: 607 us -> 0 us
  Pallas kernels: 0 us -> 147 us
  matrix products: 68.6 us -> 0 us
    dot_general x1 -> x0, blocking collectives: 607 us -> none  [step(): jnp.einsum('rsntd,rsntf->rndf', a, g, preferred_element_type=jnp.float32)]
    pallas_call x0 -> x2, Pallas kernels: none -> 147 us  [the longest x1 142 us: sum_products(): pl.pallas_call(kernel, out_shape=pltpu.VMEM((units, 2, rows, LANES), BF16...]
    dot_general x1 -> x0, matrix products: 68.6 us -> none  [step(): jnp.einsum('rsntd,rsntf->rndf', a, g, preferred_element_type=jnp.float32)]
where the time goes in v3:
time: 147 us
  Pallas kernels  147 us (100%)
    pallas_call x1, Pallas kernels, sum_products(): pl.pallas_call(kernel, out_shape=pltpu.VMEM((units, 2, rows, LANES), BF16...  142 us
    pallas_call x1, Pallas kernels, sum_products(): pl.pallas_call(store_kernel, out_shape=jax.ShapeDtypeStruct((matrices, ro...  5.3 us

profile of v3, /device:TPU:0, one launch (start us, length us, event | category | flops | bytes accessed | tf_op | source)
XLA Modules:
  0.0 146.9 jit_solution(11756102959216755959)
XLA Ops:
  0.0 141.6 %sum_of_products.1.sums = bf16[26,2,1024,128]{3,2,1,0:T(8,128)(2,1)S(1)} custom-call(bf16[1,2,4096,1024]{3,2,1,0:T(8,128)(2,1)} %a_hbm.1, bf16[1,2,4096,3328]{3,2,1,0:T(8,128)(2,1)} %g_hbm.1), custom_call_target="tpu_custom_call" | custom-call | tf_op jit(solution)/shard_map/sum_of_products/pallas_call | solution.py:306
  141.6 5.3 %store.1 = bf16[2,1024,3328]{2,1,0:T(8,128)(2,1)} custom-call(bf16[26,2,1024,128]{3,2,1,0:T(8,128)(2,1)S(1)} %sum_of_products.1.sums), custom_call_target="tpu_custom_call" | custom-call | tf_op jit(solution)/shard_map/store/pallas_call | solution.py:333
